TPU v7x, 8 devices: a whole 2x2x1 slice. The times are simulated.
8 devices in a mesh: part: 1 (over z), tp: 2 (over y), dp: 4 (over x, core).
Axes of the slice: x: 2, y: 2, z: 1, core: 2. Of those that a mesh axis runs over, the one named last changes fastest.
Arguments:
- features: bfloat16 [256, 196, 768], P(('part', 'tp', 'dp'))
- img_pos: int32 [48, 768], P(('part', 'dp'))
- token_ids: int32 [48, 768], P(('part', 'dp'))
- embedding: bfloat16 [50304, 1024], P('tp')
- conn_ln_w: bfloat16 [3072], replicated
- conn_ln_b: bfloat16 [3072], replicated
- conn_w1: bfloat16 [3072, 8192], replicated
- conn_b1: bfloat16 [8192], replicated
- conn_w2: bfloat16 [4096, 1024], replicated
- conn_b2: bfloat16 [1024], replicated
- ln_w: bfloat16 [1024], replicated
- w_q: bfloat16 [1024, 16, 64], P(None, 'tp')
- w_k: bfloat16 [1024, 16, 64], P(None, 'tp')
- w_v: bfloat16 [1024, 16, 64], P(None, 'tp')
- w_o: bfloat16 [16, 64, 1024], P('tp')
- w_gate: bfloat16 [1024, 4096], P(None, 'tp')
- w_up: bfloat16 [1024, 4096], P(None, 'tp')
- w_down: bfloat16 [4096, 1024], P('tp')
Outputs:
- output: bfloat16 [48, 768, 1024], P(('part', 'dp'))
All inputs are finite; a program needn't handle non-finite values.
Results may differ from a plain program's by a relative error of at most 0.00932157.
Values are sent between devices in bfloat16 or wider.
A program may use at most 1 GiB of HBM per device.

v0:
```python
import math
import jax
import jax.numpy as jnp
from jax import lax
from jax.sharding import PartitionSpec as P

ROPE_THETA = 50000.0
CONN_EPS = 1e-6
LAYER_EPS = 1e-5
QUERY_ROWS = 256

IN_SPECS = (P(('part', 'tp', 'dp'), None, None), P(('part', 'dp'), None), P(('part', 'dp'), None), P('tp', None),
            P(None), P(None), P(None, None), P(None), P(None, None), P(None), P(None),
            P(None, 'tp', None), P(None, 'tp', None), P(None, 'tp', None), P('tp', None, None),
            P(None, 'tp'), P(None, 'tp'), P('tp', None))
OUT_SPEC = P(('part', 'dp'), None, None)


def normalize(values, epsilon):
    base = values.astype(jnp.float32)
    centered = base - jnp.mean(base, axis=-1, keepdims=True)
    variance = jnp.mean(centered * centered, axis=-1, keepdims=True)
    return centered * lax.rsqrt(variance + epsilon)


def connector(features, conn_ln_w, conn_ln_b, conn_w1, conn_b1, conn_w2, conn_b2):
    tiles, patches, vis_width = features.shape
    half = math.isqrt(patches) // 2
    merged = features.reshape(tiles, half, 2, half, 2, vis_width).transpose(0, 1, 3, 2, 4, 5)
    merged = merged.reshape(tiles * half * half, 4 * vis_width)
    normed = (normalize(merged, CONN_EPS) * conn_ln_w.astype(jnp.float32) + conn_ln_b.astype(jnp.float32)).astype(jnp.bfloat16)
    hidden = jnp.dot(normed, conn_w1, preferred_element_type=jnp.float32) + conn_b1.astype(jnp.float32)
    conn_hidden = conn_w2.shape[0]
    gated = (jax.nn.silu(hidden[:, conn_hidden:]) * hidden[:, :conn_hidden]).astype(jnp.bfloat16)
    rows = jnp.dot(gated, conn_w2, preferred_element_type=jnp.float32) + conn_b2.astype(jnp.float32)
    return rows.astype(jnp.bfloat16).reshape(tiles, half * half, conn_w2.shape[1])


def rotate(vectors, cos_t, sin_t):
    pairs = vectors.reshape(vectors.shape[:-1] + (vectors.shape[-1] // 2, 2))
    real_part = pairs[..., 0]
    imag_part = pairs[..., 1]
    turned = jnp.stack([real_part * cos_t - imag_part * sin_t, imag_part * cos_t + real_part * sin_t], axis=-1)
    return turned.reshape(vectors.shape)


def decoder_layer(hidden, ln_w, w_q, w_k, w_v, w_o, w_gate, w_up, w_down):
    batch, seq_len, d_model = hidden.shape
    kv_heads, head_dim = w_k.shape[1], w_k.shape[2]
    group_size = w_q.shape[1] // kv_heads
    normed = (normalize(hidden, LAYER_EPS) * ln_w.astype(jnp.float32)).astype(jnp.bfloat16)
    positions = jnp.arange(seq_len, dtype=jnp.float32)
    inv_freq = ROPE_THETA ** (-jnp.arange(0, head_dim, 2, dtype=jnp.float32) / head_dim)
    angles = positions[:, None] * inv_freq[None, :]
    cos_t = jnp.cos(angles)[:, None, :]
    sin_t = jnp.sin(angles)[:, None, :]
    query = rotate(jnp.einsum('btd,dhe->bthe', normed, w_q, preferred_element_type=jnp.float32), cos_t, sin_t).astype(jnp.bfloat16)
    query = query.reshape(batch, seq_len, kv_heads, group_size, head_dim)
    keys = rotate(jnp.einsum('btd,dke->btke', normed, w_k, preferred_element_type=jnp.float32), cos_t, sin_t).astype(jnp.bfloat16)
    values = jnp.einsum('btd,dke->btke', normed, w_v, preferred_element_type=jnp.float32).astype(jnp.bfloat16)
    scale = head_dim ** -0.5
    pieces = []
    for start in range(0, seq_len, QUERY_ROWS):
        stop = min(start + QUERY_ROWS, seq_len)
        scores = jnp.einsum('bqkge,bske->bkgqs', query[:, start:stop], keys[:, :stop], preferred_element_type=jnp.float32) * scale
        allowed = jnp.arange(start, stop)[:, None] >= jnp.arange(stop)[None, :]
        scores = jnp.where(allowed, scores, -jnp.inf)
        attn_probs = jax.nn.softmax(scores, axis=-1).astype(jnp.bfloat16)
        pieces.append(jnp.einsum('bkgqs,bske->bqkge', attn_probs, values[:, :stop], preferred_element_type=jnp.float32).astype(jnp.bfloat16))
    attended = jnp.concatenate(pieces, axis=1).reshape(batch, seq_len, kv_heads * group_size, head_dim)
    branch = jnp.einsum('bthe,hed->btd', attended, w_o, preferred_element_type=jnp.float32)
    gate = jnp.einsum('btd,df->btf', normed, w_gate, preferred_element_type=jnp.float32)
    up_proj = jnp.einsum('btd,df->btf', normed, w_up, preferred_element_type=jnp.float32)
    gated = (jax.nn.silu(gate) * up_proj).astype(jnp.bfloat16)
    return branch + jnp.einsum('btf,fd->btd', gated, w_down, preferred_element_type=jnp.float32)


def solution(mesh):
    def local(features, img_pos, token_ids, embedding, conn_ln_w, conn_ln_b, conn_w1, conn_b1, conn_w2, conn_b2, ln_w, w_q, w_k, w_v, w_o, w_gate, w_up, w_down):
        tile_rows = connector(features, conn_ln_w, conn_ln_b, conn_w1, conn_b1, conn_w2, conn_b2)
        d_model = tile_rows.shape[-1]
        table = lax.all_gather(tile_rows, ('tp', 'dp'), axis=0, tiled=True).reshape(-1, d_model)
        vocab_rows = embedding.shape[0]
        local_ids = token_ids - lax.axis_index('tp') * vocab_rows
        owned = (local_ids >= 0) & (local_ids < vocab_rows)
        text_rows = jnp.take(embedding, jnp.clip(local_ids, 0, vocab_rows - 1), axis=0)
        text_rows = jnp.where(owned[..., None], text_rows, jnp.zeros((), text_rows.dtype))
        text_rows = lax.psum(text_rows, 'tp')
        picked = jnp.take(table, jnp.maximum(img_pos, 0), axis=0)
        hidden = jnp.where((img_pos >= 0)[..., None], picked, text_rows)
        partial = decoder_layer(hidden, ln_w, w_q, w_k, w_v, w_o, w_gate, w_up, w_down).astype(jnp.bfloat16)
        total = lax.psum(partial, 'tp')
        return (hidden.astype(jnp.float32) + total.astype(jnp.float32)).astype(jnp.bfloat16)

    return jax.shard_map(local, mesh=mesh, in_specs=IN_SPECS, out_specs=OUT_SPEC, check_vma=False)
```

profile of v0, /device:TPU:0, one launch (start us, length us, event | category | flops | bytes accessed | tf_op | source)
XLA Modules:
  0.0 2090.5 jit_solution(4854158174018461487)
XLA Ops:
  20.1 36.3 %fusion.88 = f32[32,7,7]{2,1,0:T(8,128)S(1)} fusion(f32[32,7,2,7,2,768]{5,0,4,3,2,1:T(8,128)} %convert.21), kind=kLoop, calls=%fused_computation.121 | loop fusion | flops 4815328 | bytes 19273856 | tf_op jit(solution)/shard_map/reduce_sum | solution.py:21
  95.4 24.5 %reshape.228 = f32[1568,3072]{1,0:T(8,128)} reshape(f32[32,7,7,2,2,768]{5,4,3,2,1,0:T(2,128)} %bitcast.163) | data formatting | bytes 38535168 | tf_op jit(solution)/shard_map/convert_element_type | solution.py:20
  119.9 93.8 %convolution_add_fusion = f32[1568,8192]{1,0:T(8,128)} fusion(bf16[3072,8192]{1,0:T(8,128)(2,1)} %param.24, f32[8192]{0:T(1024)S(1)} %convert_element_type.123, f32[1568,3072]{1,0:T(8,128)} %reshape.228, f32[3072]{0:T(1024)S(1)} %convert_element_type.121, f32[3072]{0:T(1024)S(1)} %convert_element_type.120, f32[1568]{0:T(1024)S(1)} %rsqrt.20, f32[1568]{0:T(1024)S(1)} %div.67), kind=kOutput, calls=%fused_computation.27 | convolution fusion | flops 78956953600 | bytes 121049344 | tf_op jit(solution)/shard_map/dot_general | solution.py:32
  213.7 25.7 %add_convert_fusion.4 = bf16[1568,1024]{1,0:T(8,128)(2,1)} fusion(bf16[4096,1024]{1,0:T(8,128)(2,1)} %param.26, f32[1568,8192]{1,0:T(8,128)} %convolution_add_fusion, f32[1024]{0:T(1024)S(1)} %copy-done.19), kind=kOutput, calls=%fused_computation.69 | convolution fusion | flops 13195083776 | bytes 62984192 | tf_op jit(solution)/shard_map/dot_general | solution.py:35
  249.7 300.8 %gather_fusion.1 = bf16[9216,1024]{1,0:T(8,128)(2,1)} fusion(bf16[25152,1024]{1,0:T(8,128)(2,1)} %param.21, s32[9216]{0:T(1024)S(1)} %broadcast_clamp_fusion), kind=kCustom, calls=%fused_computation.1 | custom fusion | bytes 37785600 | tf_op jit(solution)/shard_map/jit(_take)/gather | solution.py:86
  572.2 27.6 %copy.28 = bf16[256,49,1024]{2,1,0:T(8,128)(2,1)} copy(bf16[256,49,1024]{2,0,1:T(8,128)(2,1)} %all-gather.2.cloned.1.call-done) | data formatting | bytes 51380224 | tf_op jit(solution)/shard_map/all_gather | solution.py:82
  599.8 33.3 %reshape.218 = bf16[12544,1024]{1,0:T(8,128)(2,1)} reshape(bf16[256,49,1024]{2,1,0:T(8,128)(2,1)} %copy.28) | data formatting | bytes 51380224 | tf_op jit(solution)/shard_map/reshape | solution.py:82
  633.2 57.3 %gather_fusion = bf16[9216,1024]{1,0:T(8,128)(2,1)} fusion(bf16[12544,1024]{1,0:T(8,128)(2,1)} %reshape.218, s32[9216]{0:T(1024)S(1)} %broadcast_clamp_fusion.1), kind=kCustom, calls=%fused_computation | custom fusion | bytes 37785600 | tf_op jit(solution)/shard_map/jit(_take)/gather | solution.py:89
  690.5 302.2 %all-reduce.3.cloned.1.call-done = bf16[12,768,1024]{2,1,0:T(8,128)(2,1)} async-done(((bf16[12,768,1024]{2,1,0:T(8,128)(2,1)}), bf16[12,768,1024]{2,1,0:T(8,128)(2,1)}) %all-reduce.3.cloned.1.call-update) | async-done | bytes 18874384 | tf_op jit(solution)/shard_map/psum | solution.py:88
  992.6 24.0 %convert_reduce_fusion = (f32[12,768]{1,0:T(8,128)S(1)}, bf16[12,768,1024]{2,1,0:T(8,128)(2,1)}) fusion(bf16[12,768,1024]{2,1,0:T(8,128)(2,1)} %all-reduce.3.cloned.1.call-done, bf16[12,768,1024]{2,1,0:T(8,128)(2,1)} %bitcast.164, pred[12,768]{1,0:T(8,128)(4,1)S(1)} %get-tuple-element.16, pred[12,768]{1,0:T(8,128)(4,1)S(1)} %get-tuple-element.15), kind=kLoop, calls=%fused_computation.10 | loop fusion | flops 37739520 | bytes 56678400 | tf_op jit(solution)/shard_map/reduce_sum | solution.py:21
  1059.6 22.4 %reshape.220 = f32[12,768,8,32,2]{1,4,3,2,0:T(2,128)} reshape(f32[12,768,8,64]{1,3,2,0:T(8,128)} %fusion.19) | data formatting | bytes 37748736 | tf_op jit(solution)/shard_map/reshape | solution.py:40
  1100.9 22.1 %reshape.219 = f32[12,768,8,32,2]{1,4,3,2,0:T(2,128)} reshape(f32[12,768,8,64]{1,3,2,0:T(8,128)} %fusion.21) | data formatting | bytes 37748736 | tf_op jit(solution)/shard_map/reshape | solution.py:40
  1123.1 54.7 %subtract_convert_fusion = (bf16[12,768,8,32,1]{1,4,3,2,0:T(2,128)(2,1)}, bf16[12,768,8,32,1]{1,4,3,2,0:T(2,128)(2,1)}, bf16[12,768,8,32,1]{1,4,3,2,0:T(2,128)(2,1)}, bf16[12,768,8,32,1]{1,4,3,2,0:T(2,128)(2,1)}) fusion(f32[12,768,8,32,2]{1,4,3,2,0:T(2,128)} %reshape.220, f32[768,32]{0,1:T(8,128)S(1)} %copy-done.7, f32[768,32]{0,1:T(8,128)S(1)} %copy-done.6, ...), kind=kLoop, calls=%fused_computation.65 | loop fusion | flops 37748736 | bytes 56819712 | tf_op jit(solution)/shard_map/convert.5
  1177.8 53.5 %pad_maximum_fusion = (bf16[12,768,8,32,2]{1,4,3,2,0:T(2,128)(2,1)}, bf16[12,768,8,32,2]{1,4,3,2,0:T(2,128)(2,1)}) fusion(bf16[12,768,8,32,1]{1,4,3,2,0:T(2,128)(2,1)} %get-tuple-element.13, bf16[12,768,8,32,1]{1,4,3,2,0:T(2,128)(2,1)} %get-tuple-element.14, bf16[12,768,8,32,1]{1,4,3,2,0:T(2,128)(2,1)} %get-tuple-element.10, ...), kind=kLoop, calls=%fused_computation.57 | loop fusion | flops 37748736 | bytes 37748736 | tf_op jit(solution)/shard_map/stack | solution.py:43
  1350.9 23.5 %convert_bitcast_fusion.1 = bf16[12,256,8,1,64]{1,4,2,0,3:T(8,128)(2,1)} fusion(f32[12,8,256]{2,1,0:T(8,128)S(1)} %fusion.4, f32[12,8,256]{2,1,0:T(8,128)S(1)} %get-tuple-element.22, f32[12,8,512,256]{3,2,1,0:T(8,128)} %get-tuple-element.23, pred[256,512]{0,1:T(8,128)(4,1)S(1)} %copy-done.4, bf16[12,768,8,64]{1,3,2,0:T(8,128)(2,1)} %fusion.40), kind=kOutput, calls=%fused_computation.85 | convolution fusion | flops 1675100160 | bytes 60096512 | tf_op jit(solution)/shard_map/bkgqs,bske->bqkge/dot_general | solution.py:69
  1374.4 30.7 %fusion.1 = (f32[12,8,256]{2,1,0:T(8,128)S(1)}, f32[12,8,768,256]{3,2,1,0:T(8,128)}) fusion(pred[256,768]{0,1:T(8,128)(4,1)S(1)} %copy-done.3, bf16[12,768,8,64]{1,3,2,0:T(8,128)(2,1)} %convert_element_type.131, bf16[12,768,8,1,64]{1,4,2,0,3:T(8,128)(2,1)} %convert_element_type.132), kind=kOutput, calls=%fused_computation.7 | convolution fusion | flops 2472517632 | bytes 88375296 | tf_op jit(solution)/shard_map/bqkge,bske->bkgqs/dot_general | solution.py:65
  1405.1 24.0 %fusion = f32[12,8,256]{2,1,0:T(8,128)S(1)} fusion(f32[12,8,768,256]{3,2,1,0:T(8,128)} %get-tuple-element.21, f32[12,8,256]{2,1,0:T(8,128)S(1)} %get-tuple-element.20, pred[256,768]{0,1:T(8,128)(4,1)S(1)} %copy-done.3), kind=kLoop, calls=%fused_computation.6 | loop fusion | flops 75472896 | bytes 75890688 | tf_op jit(solution)/shard_map/reduce_sum | solution.py:68
  1429.2 34.6 %convert_bitcast_fusion = bf16[12,256,8,1,64]{1,4,2,0,3:T(8,128)(2,1)} fusion(bf16[12,768,8,64]{1,3,2,0:T(8,128)(2,1)} %fusion.40, f32[12,8,256]{2,1,0:T(8,128)S(1)} %fusion, f32[12,8,256]{2,1,0:T(8,128)S(1)} %get-tuple-element.20, f32[12,8,768,256]{3,2,1,0:T(8,128)} %get-tuple-element.21, pred[256,768]{0,1:T(8,128)(4,1)S(1)} %copy-done.3), kind=kOutput, calls=%fused_computation.84 | convolution fusion | flops 2511863808 | bytes 88473600 | tf_op jit(solution)/shard_map/bkgqs,bske->bqkge/dot_general | solution.py:69
  1463.8 49.4 %fusion.51 = f32[12,768,2048]{2,1,0:T(8,128)} fusion(bf16[1024,2048]{1,0:T(8,128)(2,1)} %param.33, bf16[12,768,1024]{2,1,0:T(8,128)(2,1)} %get-tuple-element.6, f32[1024]{0:T(1024)S(1)} %copy-done.18, f32[12,768]{1,0:T(8,128)S(1)} %copy-done.12, f32[12,768]{1,0:T(8,128)S(1)} %copy-done.9), kind=kOutput, calls=%fused_computation.75 | convolution fusion | flops 38701891584 | bytes 98643968 | tf_op jit(solution)/shard_map/btd,df->btf/dot_general | solution.py:72
  1513.3 57.4 %multiply_convert_fusion.4 = bf16[12,768,2048]{2,1,0:T(8,128)(2,1)} fusion(f32[12,768,2048]{2,1,0:T(8,128)} %fusion.51, bf16[1024,2048]{1,0:T(8,128)(2,1)} %param.34, bf16[12,768,1024]{2,1,0:T(8,128)(2,1)} %get-tuple-element.6, f32[1024]{0:T(1024)S(1)} %copy-done.18, f32[12,768]{1,0:T(8,128)S(1)} %copy-done.12, f32[12,768]{1,0:T(8,128)S(1)} %copy-done.9), kind=kOutput, calls=%fused_computation.3.clone.clone.1 | convolution fusion | flops 38815137792 | bytes 136392704 | tf_op jit(solution)/shard_map/btd,df->btf/dot_general | solution.py:73
  1570.6 47.3 %fusion.13 = f32[12,768,1024]{2,1,0:T(8,128)} fusion(bf16[2048,1024]{1,0:T(8,128)(2,1)} %param.35, bf16[12,768,2048]{2,1,0:T(8,128)(2,1)} %multiply_convert_fusion.4), kind=kOutput, calls=%fused_computation.26 | convolution fusion | flops 38654705664 | bytes 79691776 | tf_op jit(solution)/shard_map/btf,fd->btd/dot_general | solution.py:75
  1617.9 22.6 %fusion.10 = bf16[12,768,1024]{2,1,0:T(8,128)(2,1)} fusion(f32[12,768,1024]{2,1,0:T(8,128)} %fusion.13, bf16[12,256,8,1,64]{1,4,2,0,3:T(8,128)(2,1)} %convert_bitcast_fusion, bf16[12,256,8,1,64]{1,4,2,0,3:T(8,128)(2,1)} %convert_bitcast_fusion.1, bf16[12,256,8,1,64]{1,4,2,0,3:T(8,128)(2,1)S(1)} %copy-done.23, bf16[8,64,1024]{2,1,0:T(8,128)(2,1)S(1)} %copy-done), kind=kOutput, calls=%fused_computation.23 | convolution fusion | flops 9710862336 | bytes 67108864 | tf_op jit(solution)/shard_map/bthe,hed->btd/dot_general | solution.py:71
  1640.5 418.3 %all-reduce.5.cloned.1.call-done = bf16[12,768,1024]{2,1,0:T(8,128)(2,1)} async-done(((bf16[12,768,1024]{2,1,0:T(8,128)(2,1)}), bf16[12,768,1024]{2,1,0:T(8,128)(2,1)}) %all-reduce.5.cloned.1.call-update) | async-done | bytes 18874384 | tf_op jit(solution)/shard_map/psum | solution.py:92
  2058.8 23.8 %fusion.9 = bf16[12,768,1024]{2,1,0:T(8,128)(2,1)} fusion(bf16[12,768,1024]{2,1,0:T(8,128)(2,1)} %get-tuple-element.6, bf16[12,768,1024]{2,1,0:T(8,128)(2,1)} %all-reduce.5.cloned.1.call-done), kind=kLoop, calls=%fused_computation.21 | loop fusion | flops 37748736 | bytes 56623104 | tf_op jit(solution)/shard_map/convert_element_type | solution.py:93
  (104 shorter events, 265.1 us)
Async XLA Ops:
  7.4 1610.5 %copy-start = (bf16[8,64,1024]{2,1,0:T(8,128)(2,1)S(1)}, bf16[8,64,1024]{2,1,0:T(8,128)(2,1)}, u32[]{:S(2)}) copy-start(bf16[8,64,1024]{2,1,0:T(8,128)(2,1)} %param.32) | copy-start | bytes 3145732
  7.4 564.8 %all-gather.2.cloned.1.call-start = ((), (), s32[]{:S(2)}) async-start(), calls=%async_computation | async-start | bytes 28901376 | tf_op jit(solution)/shard_map/all_gather | solution.py:82
  20.1 36.3 %copy-start.1 = (f32[32,7,2,7,2,768]{5,0,4,3,2,1:T(8,128)S(1)}, f32[32,7,2,7,2,768]{5,0,4,3,2,1:T(8,128)}, u32[]{:S(2)}) copy-start(f32[32,7,2,7,2,768]{5,0,4,3,2,1:T(8,128)} %convert.21) | copy-start | bytes 57802756
  74.2 20.3 copy-start.20
  74.2 20.9 copy-start.15
  74.2 20.9 copy-start.16
  74.3 20.9 copy-start.14
  119.9 93.8 %copy-start.19 = (f32[1024]{0:T(1024)S(1)}, f32[1024]{0:T(1024)}, u32[]{:S(2)}) copy-start(f32[1024]{0:T(1024)} %convert_element_type.125) | copy-start | bytes 12292
  213.7 35.9 %copy-start.13 = (s32[12,768]{1,0:T(8,128)S(1)}, s32[12,768]{1,0:T(8,128)}, u32[]{:S(2)}) copy-start(s32[12,768]{1,0:T(8,128)} %param.20) | copy-start | bytes 110596
  249.6 743.1 %all-reduce.3.cloned.1.call-start = ((), (), s32[]{:S(2)}) async-start(), calls=%async_computation.1 | async-start | bytes 37748736 | tf_op jit(solution)/shard_map/psum | solution.py:88
  568.0 1490.8 %all-reduce.5.cloned.1.call-start = ((), (), s32[]{:S(2)}) async-start(), calls=%async_computation.2 | async-start | bytes 37748736 | tf_op jit(solution)/shard_map/psum | solution.py:92
  568.8 513.2 %copy-start.17 = (f32[1024]{0:T(1024)}, f32[1024]{0:T(1024)S(1)}, u32[]{:S(2)}) copy-start(f32[1024]{0:T(1024)S(1)} %convert_element_type.128) | copy-start | bytes 12292
  1016.7 65.3 %copy-start.8 = (f32[12,768]{1,0:T(8,128)}, f32[12,768]{1,0:T(8,128)S(1)}, u32[]{:S(2)}) copy-start(f32[12,768]{1,0:T(8,128)S(1)} %broadcast_multiply_fusion.1) | copy-start | bytes 110596
  1028.6 53.4 %copy-start.11 = (f32[12,768]{1,0:T(8,128)}, f32[12,768]{1,0:T(8,128)S(1)}, u32[]{:S(2)}) copy-start(f32[12,768]{1,0:T(8,128)S(1)} %add_rsqrt_fusion.1) | copy-start | bytes 110596
  1059.6 22.4 %copy-start.22 = (bf16[1024,8,64]{0,2,1:T(8,128)(2,1)S(1)}, bf16[1024,8,64]{0,2,1:T(8,128)(2,1)}, u32[]{:S(2)}) copy-start(bf16[1024,8,64]{0,2,1:T(8,128)(2,1)} %param.30) | copy-start | bytes 3145732
  1100.9 22.1 %copy-start.6 = (f32[768,32]{0,1:T(8,128)S(1)}, f32[768,32]{0,1:T(8,128)}, u32[]{:S(2)}) copy-start(f32[768,32]{0,1:T(8,128)} %get-tuple-element.18) | copy-start | bytes 294916
  1100.9 22.1 %copy-start.7 = (f32[768,32]{0,1:T(8,128)S(1)}, f32[768,32]{0,1:T(8,128)}, u32[]{:S(2)}) copy-start(f32[768,32]{0,1:T(8,128)} %get-tuple-element.19) | copy-start | bytes 294916
  1231.3 40.4 %copy-start.5 = (pred[256,256]{0,1:T(8,128)(4,1)S(1)}, pred[256,256]{0,1:T(8,128)(4,1)}, u32[]{:S(2)}) copy-start(pred[256,256]{0,1:T(8,128)(4,1)} %iota_compare_fusion.2) | copy-start | bytes 196612
  1251.6 33.0 %slice-start = ((s8[9437184]{0:T(1024)(128)(4,1)}), s8[1048576]{0:T(1024)(128)(4,1)S(1)}, s32[]{:S(2)}) async-start(s8[9437184]{0:T(1024)(128)(4,1)} %bitcast.161), calls=%async_computation.3 | async-start | bytes 2097152
  1350.9 23.5 %copy-start.3 = (pred[256,768]{0,1:T(8,128)(4,1)S(1)}, pred[256,768]{0,1:T(8,128)(4,1)}, u32[]{:S(2)}) copy-start(pred[256,768]{0,1:T(8,128)(4,1)} %iota_compare_fusion) | copy-start | bytes 589828
  1429.1 34.7 %copy-start.9 = (f32[12,768]{1,0:T(8,128)S(1)}, f32[12,768]{1,0:T(8,128)}, u32[]{:S(2)}) copy-start(f32[12,768]{1,0:T(8,128)} %copy-done.8) | copy-start | bytes 110596
  1429.2 34.7 %copy-start.12 = (f32[12,768]{1,0:T(8,128)S(1)}, f32[12,768]{1,0:T(8,128)}, u32[]{:S(2)}) copy-start(f32[12,768]{1,0:T(8,128)} %copy-done.11) | copy-start | bytes 110596
  1429.2 34.6 %copy-start.18 = (f32[1024]{0:T(1024)S(1)}, f32[1024]{0:T(1024)}, u32[]{:S(2)}) copy-start(f32[1024]{0:T(1024)} %copy-done.17) | copy-start | bytes 12292
  1570.6 47.3 %copy-start.23 = (bf16[12,256,8,1,64]{1,4,2,0,3:T(8,128)(2,1)S(1)}, bf16[12,256,8,1,64]{1,4,2,0,3:T(8,128)(2,1)}, u32[]{:S(2)}) copy-start(bf16[12,256,8,1,64]{1,4,2,0,3:T(8,128)(2,1)} %convert_bitcast_fusion.2) | copy-start | bytes 9437188
  (6 other events, 52.4 us)
Sparse Core Ops, SparseCore 0:
  249.7 124.6 all-gather.1
Sparse Core Ops, SparseCore 1:
  568.1 424.5 all-reduce.2
  1640.6 418.1 all-reduce.4
where the time goes:
time: 2110 us; the launch traced here: 2090 us
  waiting for transfers between devices  721 us (34%)
  local copies, waits for them, and re-layouts  563 us (27%)
  matrix products  482 us (23%)
  other arithmetic  310 us (15%)
    psum x1, waiting for transfers between devices, local(): total = lax.psum(partial, 'tp')  418 us
    psum x1, waiting for transfers between devices, local(): text_rows = lax.psum(text_rows, 'tp')  302 us
    gather x1, local copies, waits for them, and re-layouts, local(): jnp.take(embedding, jnp.clip(local_ids, 0, vocab_rows - 1), axis=0)  301 us
    dot_general x1, matrix products, connector(): jnp.dot(normed, conn_w1, preferred_element_type=jnp.float32)  93.8 us
    dot_general x3, matrix products, decoder_layer(): jnp.einsum('bkgqs,bske->bqkge', attn_probs, values[:, :stop], preferred_e...  72.2 us
    dot_general x3, matrix products, decoder_layer(): jnp.einsum('bqkge,bske->bkgqs', query[:, start:stop], keys[:, :stop], pre...  63.5 us
    reduce_sum x2, other arithmetic, normalize(): centered = base - jnp.mean(base, axis=-1, keepdims=True)  60.3 us
    dot_general x1, matrix products, decoder_layer(): jnp.einsum('btd,df->btf', normed, w_up, preferred_element_type=jnp.float32)  57.4 us
  transfers between devices with their start and end apart: 3, of which 2 were waited for; matrix products, arithmetic and copies ran while one was open for 21% of the time, Pallas kernels for 0%

commit v1 on v0

v1 whole, which is shorter than its diff:
```python
import math
import jax
import jax.numpy as jnp
from jax import lax
from jax.experimental import pallas as pl
from jax.experimental.pallas import tpu as pltpu
from jax.sharding import PartitionSpec as P

ROPE_THETA = 50000.0
CONN_EPS = 1e-6
LAYER_EPS = 1e-5
QUERY_ROWS = 256
LANES = 128
CHUNKS = (3, 2, 1)

IN_SPECS = (P(('part', 'tp', 'dp'), None, None), P(('part', 'dp'), None), P(('part', 'dp'), None), P('tp', None),
            P(None), P(None), P(None, None), P(None), P(None, None), P(None), P(None),
            P(None, 'tp', None), P(None, 'tp', None), P(None, 'tp', None), P('tp', None, None),
            P(None, 'tp'), P(None, 'tp'), P('tp', None))
OUT_SPEC = P(('part', 'dp'), None, None)
SWAP = [(0, 1), (1, 0)]


def normalize(values, epsilon):
    base = values.astype(jnp.float32)
    centered = base - jnp.mean(base, axis=-1, keepdims=True)
    variance = jnp.mean(centered * centered, axis=-1, keepdims=True)
    return centered * lax.rsqrt(variance + epsilon)


def connector(features, after, conn_ln_w, conn_ln_b, conn_w1, conn_b1, conn_w2, conn_b2):
    tiles, patches, vis_width = features.shape
    half = math.isqrt(patches) // 2
    merged = features.reshape(tiles, half, 2, half, 2, vis_width).transpose(0, 1, 3, 2, 4, 5)
    merged = lax.optimization_barrier(merged.reshape(tiles * half * half, 4 * vis_width))
    normed = (normalize(merged, CONN_EPS) * conn_ln_w.astype(jnp.float32) + conn_ln_b.astype(jnp.float32)).astype(jnp.bfloat16)
    normed, after = lax.optimization_barrier((normed, after))
    hidden = jnp.dot(normed, conn_w1, preferred_element_type=jnp.float32) + conn_b1.astype(jnp.float32)
    conn_hidden = conn_w2.shape[0]
    gated = (jax.nn.silu(hidden[:, conn_hidden:]) * hidden[:, :conn_hidden]).astype(jnp.bfloat16)
    rows = jnp.dot(gated, conn_w2, preferred_element_type=jnp.float32) + conn_b2.astype(jnp.float32)
    return rows.astype(jnp.bfloat16), after


def attention_kernel(head_dim, q_ref, k_ref, v_ref, cos_ref, sin_ref, out_ref):
    seq_len, width = q_ref.shape[1], q_ref.shape[2]
    cos_t, sin_t = cos_ref[...], sin_ref[...]
    lane = lax.broadcasted_iota(jnp.int32, (seq_len, width), 1)
    even = lane % 2 == 0

    def rotate(vectors):
        partner = jnp.where(even, pltpu.roll(vectors, width - 1, 1), pltpu.roll(vectors, 1, 1))
        return vectors * cos_t + partner * sin_t

    query = rotate(q_ref[0]).astype(jnp.bfloat16) * jnp.asarray(head_dim ** -0.5, jnp.bfloat16)
    keys = rotate(k_ref[0]).astype(jnp.bfloat16)
    values_t = v_ref[0].T.astype(jnp.bfloat16)
    heads = width // head_dim
    row = lax.broadcasted_iota(jnp.int32, (QUERY_ROWS, QUERY_ROWS), 0)
    column = lax.broadcasted_iota(jnp.int32, (QUERY_ROWS, QUERY_ROWS), 1)
    allowed = jnp.concatenate([row <= column] * heads, axis=1)
    out_lane = lax.broadcasted_iota(jnp.int32, (QUERY_ROWS, width), 1)
    masks = [(out_lane >= head * head_dim) & (out_lane < (head + 1) * head_dim) for head in range(heads)]
    out_row = lax.broadcasted_iota(jnp.int32, (width, QUERY_ROWS), 0)
    for start in range(0, seq_len, QUERY_ROWS):
        stop = start + QUERY_ROWS
        part = query[start:stop].astype(jnp.float32)
        block = jnp.concatenate([jnp.where(mine, part, 0.0) for mine in masks], axis=0).astype(jnp.bfloat16)
        scores = lax.dot_general(keys[:stop], block, (((1,), (1,)), ((), ())), preferred_element_type=jnp.float32)
        diagonal = jnp.where(allowed, scores[start:], -jnp.inf)
        scores = diagonal if start == 0 else jnp.concatenate([scores[:start], diagonal], axis=0)
        weights = jnp.exp(scores - jnp.max(scores, axis=0, keepdims=True))
        weights = (weights * (1.0 / jnp.sum(weights, axis=0, keepdims=True))).astype(jnp.bfloat16)
        product = lax.dot_general(values_t[:, :stop], weights, (((1,), (0,)), ((), ())), preferred_element_type=jnp.float32)
        result = product[:, :QUERY_ROWS]
        for head in range(1, heads):
            result = jnp.where(out_row >= head * head_dim, product[:, head * QUERY_ROWS:(head + 1) * QUERY_ROWS], result)
        result = result.T
        out_ref[0, start:stop, :] = result.astype(jnp.bfloat16)


def attention(qkv, cos_t, sin_t, head_dim):
    batch, seq_len, total = qkv.shape
    width = total // 3
    groups = width // LANES

    def spec(offset):
        return pl.BlockSpec((1, seq_len, LANES), lambda b, g: (b, 0, offset + g))

    table = pl.BlockSpec((seq_len, LANES), lambda b, g: (0, 0))

    def kernel(*refs):
        attention_kernel(head_dim, *refs)

    pairs = batch * width // head_dim * seq_len * seq_len
    return pl.pallas_call(
        kernel,
        name='attention',
        grid=(batch, groups),
        out_shape=jax.ShapeDtypeStruct((batch, seq_len, width), jnp.bfloat16),
        in_specs=[spec(0), spec(groups), spec(2 * groups), table, table],
        out_specs=spec(0),
        compiler_params=pltpu.CompilerParams(dimension_semantics=('parallel', 'parallel'), vmem_limit_bytes=48 * 1024 * 1024),
        cost_estimate=pl.CostEstimate(flops=pairs * head_dim * 4, bytes_accessed=batch * seq_len * width * 14, transcendentals=pairs),
    )(qkv, qkv, qkv, cos_t, sin_t)


def rope_tables(seq_len, head_dim):
    positions = jnp.arange(seq_len, dtype=jnp.float32)
    inv_freq = ROPE_THETA ** (-jnp.arange(0, head_dim, 2, dtype=jnp.float32) / head_dim)
    angles = positions[:, None] * inv_freq[None, :]
    copies = LANES // head_dim
    cos_t = jnp.tile(jnp.repeat(jnp.cos(angles), 2, axis=1), (1, copies))
    sign = jnp.where(jnp.arange(LANES) % 2 == 0, -1.0, 1.0).astype(jnp.float32)
    sin_t = jnp.tile(jnp.repeat(jnp.sin(angles), 2, axis=1), (1, copies)) * sign
    return lax.optimization_barrier((cos_t, sin_t))


def decoder_layer(hidden, ln_w, shards, cos_t, sin_t, head_dim):
    batch, seq_len, d_model = hidden.shape
    normed = (normalize(hidden, LAYER_EPS) * ln_w.astype(jnp.float32)).astype(jnp.bfloat16)
    normed = lax.optimization_barrier(normed.reshape(batch * seq_len, d_model))
    total = hidden.reshape(batch * seq_len, d_model).astype(jnp.float32)
    for w_qkv, w_gate, w_up, w_o, w_down in shards:
        qkv = jnp.dot(normed, w_qkv, preferred_element_type=jnp.float32)
        attended = attention(qkv.reshape(batch, seq_len, -1), cos_t, sin_t, head_dim)
        total = total + jnp.dot(attended.reshape(batch * seq_len, -1), w_o, preferred_element_type=jnp.float32)
        gate = jnp.dot(normed, w_gate, preferred_element_type=jnp.float32)
        up_proj = jnp.dot(normed, w_up, preferred_element_type=jnp.float32)
        gated = (jax.nn.silu(gate) * up_proj).astype(jnp.bfloat16)
        total = total + jnp.dot(gated, w_down, preferred_element_type=jnp.float32)
    return total.astype(jnp.bfloat16).reshape(batch, seq_len, d_model)


def part_from_peer(shard, copies):
    part = shard.shape[0] // copies
    mine = lax.dynamic_slice_in_dim(shard, lax.axis_index('dp') * part, part, axis=0)
    return lax.ppermute(mine, 'tp', SWAP)


def solution(mesh):
    dp = mesh.shape['dp']

    def local(features, img_pos, token_ids, embedding, conn_ln_w, conn_ln_b, conn_w1, conn_b1, conn_w2, conn_b2, ln_w, w_q, w_k, w_v, w_o, w_gate, w_up, w_down):
        d_model, heads, head_dim = w_q.shape
        width, ff = heads * head_dim, w_gate.shape[1]
        batch, seq_len = token_ids.shape
        tp = lax.axis_index('tp')
        vocab_rows = embedding.shape[0]

        w_in = jnp.concatenate([w_q.reshape(d_model, width), w_k.reshape(d_model, width), w_v.reshape(d_model, width), w_gate, w_up], axis=1)
        w_out = jnp.concatenate([w_o.reshape(width, d_model), w_down], axis=0)
        part_in, part_out = part_from_peer(w_in, dp), part_from_peer(w_out, dp)

        own_rows, peer_rows, first = [], [], 0
        for size in CHUNKS:
            own_rows.append(first + tp * size + jnp.arange(size))
            peer_rows.append(first + (1 - tp) * size + jnp.arange(size))
            first += 2 * size
        own_rows, peer_rows = jnp.concatenate(own_rows), jnp.concatenate(peer_rows)
        own_ids = jnp.take(token_ids, own_rows, axis=0) - tp * vocab_rows
        peer_ids = jnp.take(token_ids, peer_rows, axis=0) - tp * vocab_rows
        own_pos = jnp.take(img_pos, own_rows, axis=0)

        split = vocab_rows // 2
        lower, upper = lax.optimization_barrier((embedding[:split], embedding[split:]))

        def text_rows(ids):
            flat = ids.reshape(-1)
            low = jnp.take(lower, jnp.clip(flat, 0, split - 1), axis=0)
            high = jnp.take(upper, jnp.clip(flat - split, 0, vocab_rows - split - 1), axis=0)
            return jnp.where((flat < split)[:, None], low, high)

        sent = text_rows(peer_ids)
        features, sent, part_in, part_out = lax.optimization_barrier((features, sent, part_in, part_out))
        received = lax.ppermute(sent, 'tp', SWAP)
        conn_params = (conn_ln_w, conn_ln_b, conn_w1, conn_b1, conn_w2, conn_b2)
        tiles = features.shape[0] // 2
        rows_a, rest = connector(features[:tiles], features[tiles:], *conn_params)
        table_a = lax.all_gather(rows_a, ('tp', 'dp'), axis=0, tiled=True)
        rows_b, own_ids = connector(rest, own_ids, *conn_params)
        rows_b, own_ids, received, part_in, part_out = lax.optimization_barrier((rows_b, own_ids, received, part_in, part_out))
        table_b = lax.all_gather(rows_b, ('tp', 'dp'), axis=0, tiled=True)
        table_b, part_in, part_out = lax.optimization_barrier((table_b, part_in, part_out))
        peer_in = lax.all_gather(part_in, 'dp', axis=0, tiled=True)
        peer_out = lax.all_gather(part_out, 'dp', axis=0, tiled=True)
        shards = []
        for big_in, big_out in ((w_in, w_out), (peer_in, peer_out)):
            shards.append((big_in[:, :3 * width], big_in[:, 3 * width:3 * width + ff], big_in[:, 3 * width + ff:], big_out[:width], big_out[width:]))

        kept = text_rows(own_ids)
        half = rows_a.shape[0]
        flat_pos = jnp.maximum(own_pos, 0).reshape(-1)
        owner, offset = flat_pos // (2 * half), flat_pos % (2 * half)
        from_a = jnp.take(table_a, owner * half + jnp.minimum(offset, half - 1), axis=0)
        from_b = jnp.take(table_b, owner * half + jnp.maximum(offset - half, 0), axis=0)
        picked = jnp.where((offset < half)[:, None], from_a, from_b)
        owned = ((own_ids >= 0) & (own_ids < vocab_rows)).reshape(-1, 1)
        is_image = (own_pos >= 0).reshape(-1, 1)
        hidden = jnp.where(is_image, picked, jnp.where(owned, kept, received))
        hidden = lax.optimization_barrier(hidden).reshape(-1, seq_len, d_model)

        cos_t, sin_t = rope_tables(seq_len, head_dim)
        whole, first = jnp.zeros((batch, seq_len, d_model), hidden.dtype), 0
        for size in CHUNKS:
            piece = decoder_layer(hidden[first:first + size], ln_w, shards, cos_t, sin_t, head_dim)
            piece = lax.all_gather(piece, 'tp', axis=0, tiled=True)
            whole = lax.dynamic_update_slice_in_dim(whole, piece, 2 * first, axis=0)
            first += size
        return whole

    return jax.shard_map(local, mesh=mesh, in_specs=IN_SPECS, out_specs=OUT_SPEC, check_vma=False)
```

time: 2110 us -> 1180 us (0.56)
  waiting for transfers between devices: 721 us -> 269 us
  local copies, waits for them, and re-layouts: 563 us -> 313 us
  other arithmetic: 310 us -> 61.1 us
  Pallas kernels: 0 us -> 104 us
  matrix products: 482 us -> 408 us
    psum x2 -> x0, waiting for transfers between devices: 720 us -> none  [the longest x1 418 us: local(): total = lax.psum(partial, 'tp')]
    ppermute x0 -> x3, waiting for transfers between devices: none -> 176 us  [the longest x1 176 us: local(): received = lax.ppermute(sent, 'tp', SWAP)]
    gather x2 -> x9, local copies, waits for them, and re-layouts: 358 us -> 187 us  [the longest x2 66.7 us: text_rows(): low = jnp.take(lower, jnp.clip(flat, 0, split - 1), axis=0)]
    another operation x2 -> x0, other arithmetic: 108 us -> none
    pallas_call x0 -> x6, Pallas kernels: none -> 104 us  [attention(): pl.pallas_call(kernel, name='attention', grid=(batch, groups), out_shape=...]
    all_gather x1 -> x7, waiting for transfers between devices: 0.02 us -> 92.1 us  [the longest x3 92.1 us: local(): piece = lax.all_gather(piece, 'tp', axis=0, tiled=True)]
    convert_element_type x4 -> x0, local copies, waits for them, and re-layouts: 84.9 us -> none  [the longest x2 44.5 us: normalize(): base = values.astype(jnp.float32)]
    dot_general x13 -> x25, matrix products: 362 us -> 288 us  [the longest x6 132 us: decoder_layer(): total = total + jnp.dot(gated, w_down, preferred_element_type=jnp.float32)]
  transfers between devices with their start and end apart: 3 -> 10, of which waited for: 2 -> 3; matrix products, arithmetic and copies ran while one was open for 21% -> 49% of each run, Pallas kernels for 0% -> 9%
where the time goes in v1:
time: 1180 us; the launch traced here: 1170 us
  matrix products  408 us (35%)
  local copies, waits for them, and re-layouts  313 us (27%)
  waiting for transfers between devices  269 us (23%)
  Pallas kernels  104 us (9%)
  other arithmetic  61.1 us (5%)
  between operations  14.9 us (1%)
    ppermute x1, waiting for transfers between devices, local(): received = lax.ppermute(sent, 'tp', SWAP)  176 us
    dot_general x6, matrix products, decoder_layer(): total = total + jnp.dot(gated, w_down, preferred_element_type=jnp.float32)  132 us
    pallas_call x6, Pallas kernels, attention(): pl.pallas_call(kernel, name='attention', grid=(batch, groups), out_shape=...  104 us
    dot_general x2, matrix products, connector(): jnp.dot(normed, conn_w1, preferred_element_type=jnp.float32)  93.8 us
    all_gather x3, waiting for transfers between devices, local(): piece = lax.all_gather(piece, 'tp', axis=0, tiled=True)  92.1 us
    gather x2, local copies, waits for them, and re-layouts, text_rows(): low = jnp.take(lower, jnp.clip(flat, 0, split - 1), axis=0)  66.7 us
    gather x2, local copies, waits for them, and re-layouts, text_rows(): jnp.take(upper, jnp.clip(flat - split, 0, vocab_rows - split - 1), axis=0)  65.1 us
    dot_general x6, matrix products, decoder_layer(): gate = jnp.dot(normed, w_gate, preferred_element_type=jnp.float32)  60.6 us
  transfers between devices with their start and end apart: 10, of which 3 were waited for; matrix products, arithmetic and copies ran while one was open for 49% of the time, Pallas kernels for 9%

profile of v1, /device:TPU:0, one launch (start us, length us, event | category | flops | bytes accessed | tf_op | source)
XLA Modules:
  0.0 1174.8 jit_solution(16044705728835505139)
XLA Ops:
  30.9 34.1 %fusion.100 = (bf16[12576,1024]{1,0:T(8,128)(2,1)}, bf16[12576,1024]{1,0:T(8,128)(2,1)}) fusion(bf16[25152,1024]{1,0:T(8,128)(2,1)} %param.27), kind=kLoop, calls=%fused_computation.201 | loop fusion | bytes 103022592 | tf_op jit(solution)/shard_map/slice | solution.py:166
  65.8 32.3 %gather_fusion.2 = bf16[4608,1024]{1,0:T(8,128)(2,1)} fusion(bf16[12576,1024]{1,0:T(8,128)(2,1)} %get-tuple-element.28, s32[5120]{0:T(1024)S(1)} %pad_clamp_fusion.5), kind=kCustom, calls=%fused_computation.1.clone | custom fusion | bytes 18892800 | tf_op jit(solution)/shard_map/jit(_take)/gather | solution.py:170
  98.2 32.5 %gather_fusion.3 = bf16[4608,1024]{1,0:T(8,128)(2,1)} fusion(bf16[12576,1024]{1,0:T(8,128)(2,1)} %get-tuple-element.29, s32[5120]{0:T(1024)S(1)} %pad_clamp_fusion.4), kind=kCustom, calls=%fused_computation.5.clone | custom fusion | bytes 18892800 | tf_op jit(solution)/shard_map/jit(_take)/gather | solution.py:171
  180.2 45.8 %convolution_add_fusion.1 = f32[784,8192]{1,0:T(8,128)} fusion(bf16[784,3072]{1,0:T(8,128)(2,1)S(1)} %fusion.17, bf16[3072,8192]{1,0:T(8,128)(2,1)} %param.30, f32[8192]{0:T(1024)S(1)} %convert_element_type.107), kind=kOutput, calls=%fused_computation.17 | convolution fusion | flops 39466434560 | bytes 80871424 | tf_op jit(solution)/shard_map/dot_general | solution.py:38
  270.2 47.9 %convolution_add_fusion = f32[784,8192]{1,0:T(8,128)} fusion(bf16[784,3072]{1,0:T(8,128)(2,1)S(1)} %fusion.13, bf16[3072,8192]{1,0:T(8,128)(2,1)} %param.30, f32[8192]{0:T(1024)S(1)} %convert_element_type.107), kind=kOutput, calls=%fused_computation.16 | convolution fusion | flops 39466434560 | bytes 80871424 | tf_op jit(solution)/shard_map/dot_general | solution.py:38
  331.4 176.4 %collective-permute-done.2 = bf16[4608,1024]{1,0:T(8,128)(2,1)} collective-permute-done((bf16[4608,1024]{1,0:T(8,128)(2,1)}, bf16[4608,1024]{1,0:T(8,128)(2,1)}, u32[]{:S(2)}, u32[]{:S(2)}) %collective-permute-start.2) | collective-permute-done | bytes 9437216 | tf_op jit(solution)/shard_map/ppermute | solution.py:176
  509.6 34.4 %gather_fusion.7 = bf16[4608,1024]{1,0:T(8,128)(2,1)} fusion(bf16[12576,1024]{1,0:T(8,128)(2,1)} %get-tuple-element.28, s32[5120]{0:T(1024)S(1)} %pad_clamp_fusion.1), kind=kCustom, calls=%fused_computation.6.clone | custom fusion | bytes 18892800 | tf_op jit(solution)/shard_map/jit(_take)/gather | solution.py:170
  544.0 32.6 %gather_fusion.8 = bf16[4608,1024]{1,0:T(8,128)(2,1)} fusion(bf16[12576,1024]{1,0:T(8,128)(2,1)} %get-tuple-element.29, s32[5120]{0:T(1024)S(1)} %pad_clamp_fusion), kind=kCustom, calls=%fused_computation.7.clone | custom fusion | bytes 18892800 | tf_op jit(solution)/shard_map/jit(_take)/gather | solution.py:171
  576.7 27.0 %gather_fusion.4 = bf16[4608,1024]{1,0:T(8,128)(2,1)} fusion(bf16[6272,1024]{1,0:T(8,128)(2,1)} %all-gather.9.cloned.1.call-done, s32[5120]{0:T(1024)S(1)} %pad_clamp_fusion.3), kind=kCustom, calls=%fused_computation.2.clone | custom fusion | bytes 18892800 | tf_op jit(solution)/shard_map/jit(_take)/gather | solution.py:195
  603.7 27.0 %gather_fusion.6 = bf16[4608,1024]{1,0:T(8,128)(2,1)} fusion(bf16[6272,1024]{1,0:T(8,128)(2,1)} %all-gather.11.cloned.1.call-done, s32[5120]{0:T(1024)S(1)} %pad_clamp_fusion.2), kind=kCustom, calls=%fused_computation.8.clone | custom fusion | bytes 18892800 | tf_op jit(solution)/shard_map/jit(_take)/gather | solution.py:196
  630.7 15.3 %fusion.26 = bf16[4608,1024]{1,0:T(8,128)(2,1)S(1)} fusion(bf16[4608,1024]{1,0:T(8,128)(2,1)} %collective-permute-done.2, bf16[4608,1024]{1,0:T(8,128)(2,1)} %gather_fusion.8, bf16[4608,1024]{1,0:T(8,128)(2,1)} %gather_fusion.7, bf16[4608,1024]{1,0:T(8,128)(2,1)} %gather_fusion.6, bf16[4608,1024]{1,0:T(8,128)(2,1)} %gather_fusion.4, ...), kind=kLoop, calls=%fused_computation.54 | loop fusion | flops 37748736 | bytes 56659968 | tf_op jit(solution)/shard_map/jit(_where)/select_n | solution.py:200
  686.6 17.4 %attention.8 = bf16[2,768,512]{2,1,0:T(8,128)(2,1)S(1)} custom-call(f32[2,768,1536]{2,1,0:T(8,128)} %bitcast.101, f32[2,768,1536]{2,1,0:T(8,128)} %bitcast.102, f32[2,768,1536]{2,1,0:T(8,128)} %bitcast.103, f32[768,128]{1,0:T(8,128)S(1)} %copy.40.refs_3_, f32[768,128]{1,0:T(8,128)S(1)} %broadcast_multiply_fusion.refs_4_), custom_call_target="tpu_custom_call" | custom-call | flops 2415919104 | bytes 11010048 | tf_op jit(solution)/shard_map/attention/pallas_call | solution.py:96
  716.4 25.2 %attention.6 = bf16[3,768,512]{2,1,0:T(8,128)(2,1)S(1)} custom-call(f32[3,768,1536]{2,1,0:T(8,128)} %bitcast.95, f32[3,768,1536]{2,1,0:T(8,128)} %bitcast.96, f32[3,768,1536]{2,1,0:T(8,128)} %bitcast.97, f32[768,128]{1,0:T(8,128)S(1)} %copy.40.refs_3_, f32[768,128]{1,0:T(8,128)S(1)} %broadcast_multiply_fusion.refs_4_), custom_call_target="tpu_custom_call" | custom-call | flops 3623878656 | bytes 16515072 | tf_op jit(solution)/shard_map/attention/pallas_call | solution.py:96
  776.5 28.9 %fusion = f32[2304,1024]{1,0:T(8,128)} fusion(bf16[2048,1024]{1,0:T(8,128)(2,1)} %param.41, f32[2304,2048]{1,0:T(8,128)} %fusion.103, bf16[2304,1024]{1,0:T(8,128)(2,1)} %copy-done.7, bf16[1024,2048]{1,0:T(8,128)(2,1)} %param.40), kind=kOutput, calls=%fused_computation.14 | convolution fusion | flops 19355664384 | bytes 41418752 | tf_op jit(solution)/shard_map/dot_general | solution.py:131
  805.7 26.3 %fusion.106 = f32[1536,1024]{1,0:T(8,128)} fusion(bf16[2048,1024]{1,0:T(8,128)(2,1)} %param.41, f32[1536,2048]{1,0:T(8,128)} %fusion.105, bf16[1536,1024]{1,0:T(8,128)(2,1)} %copy-done.14, bf16[1024,2048]{1,0:T(8,128)(2,1)} %param.40), kind=kOutput, calls=%fused_computation.207 | convolution fusion | flops 12903776256 | bytes 30408704 | tf_op jit(solution)/shard_map/dot_general | solution.py:131
  832.0 13.7 %fusion.70 = f32[2304,1536]{1,0:T(8,128)} fusion(bf16[2304,1024]{1,0:T(8,128)(2,1)} %copy-done.7, bf16[1024,5632]{1,0:T(8,128)(2,1)} %all-gather.13.cloned.1.call-done), kind=kOutput, calls=%fused_computation.110 | convolution fusion | flops 7247757312 | bytes 22020096 | tf_op jit(solution)/shard_map/dot_general | solution.py:125
  845.8 25.3 %attention.7 = bf16[3,768,512]{2,1,0:T(8,128)(2,1)S(1)} custom-call(f32[3,768,1536]{2,1,0:T(8,128)} %bitcast.98, f32[3,768,1536]{2,1,0:T(8,128)} %bitcast.99, f32[3,768,1536]{2,1,0:T(8,128)} %bitcast.100, f32[768,128]{1,0:T(8,128)S(1)} %copy.40.refs_3_, f32[768,128]{1,0:T(8,128)S(1)} %broadcast_multiply_fusion.refs_4_), custom_call_target="tpu_custom_call" | custom-call | flops 3623878656 | bytes 16515072 | tf_op jit(solution)/shard_map/attention/pallas_call | solution.py:96
  871.1 15.5 %fusion.58 = f32[2304,2048]{1,0:T(8,128)} fusion(bf16[2304,1024]{1,0:T(8,128)(2,1)S(1)} %copy-done.8, bf16[1024,5632]{1,0:T(8,128)(2,1)} %all-gather.13.cloned.1.call-done), kind=kOutput, calls=%fused_computation.97 | convolution fusion | flops 9663676416 | bytes 27787264 | tf_op jit(solution)/shard_map/dot_general | solution.py:128
  892.9 32.2 %fusion.24 = bf16[2304,1024]{1,0:T(8,128)(2,1)} fusion(f32[2304,1024]{1,0:T(8,128)} %fusion.80, f32[2304,1024]{1,0:T(8,128)} %fusion, f32[2304,1024]{1,0:T(8,128)} %fusion.102, f32[2304,2048]{1,0:T(8,128)} %fusion.58, bf16[2304,1024]{1,0:T(8,128)(2,1)} %copy-done.7, bf16[2560,1024]{1,0:T(8,128)(2,1)} %all-gather.15.cloned.1.call-done, ...), kind=kOutput, calls=%fused_computation.51 | convolution fusion | flops 19369820160 | bytes 69730304 | tf_op jit(solution)/shard_map/dot_general | solution.py:131
  942.9 17.3 %attention.9 = bf16[2,768,512]{2,1,0:T(8,128)(2,1)S(1)} custom-call(f32[2,768,1536]{2,1,0:T(8,128)} %bitcast.104, f32[2,768,1536]{2,1,0:T(8,128)} %bitcast.105, f32[2,768,1536]{2,1,0:T(8,128)} %bitcast.106, f32[768,128]{1,0:T(8,128)S(1)} %copy.40.refs_3_, f32[768,128]{1,0:T(8,128)S(1)} %broadcast_multiply_fusion.refs_4_), custom_call_target="tpu_custom_call" | custom-call | flops 2415919104 | bytes 11010048 | tf_op jit(solution)/shard_map/attention/pallas_call | solution.py:96
  971.6 24.5 %fusion.46 = f32[1536,1024]{1,0:T(8,128)} fusion(bf16[2560,1024]{1,0:T(8,128)(2,1)} %all-gather.15.cloned.1.call-done, f32[1536,2048]{1,0:T(8,128)} %fusion.56, bf16[1536,1024]{1,0:T(8,128)(2,1)} %copy-done.14, bf16[1024,5632]{1,0:T(8,128)(2,1)} %all-gather.13.cloned.1.call-done), kind=kOutput, calls=%fused_computation.87 | convolution fusion | flops 12903776256 | bytes 30408704 | tf_op jit(solution)/shard_map/dot_general | solution.py:131
  1006.8 14.1 %fusion.72 = f32[768,1024]{1,0:T(8,128)} fusion(bf16[2048,1024]{1,0:T(8,128)(2,1)} %param.41, f32[768,2048]{1,0:T(8,128)} %fusion.107, bf16[768,1024]{1,0:T(8,128)(2,1)} %copy-done.17, bf16[1024,2048]{1,0:T(8,128)(2,1)} %param.40), kind=kOutput, calls=%fused_computation.112 | convolution fusion | flops 6451888128 | bytes 19398656 | tf_op jit(solution)/shard_map/dot_general | solution.py:131
  1065.2 54.8 %all-gather.19.cloned.1.call-done = bf16[4,768,1024]{2,1,0:T(8,128)(2,1)} async-done(((bf16[2,768,1024]{2,1,0:T(8,128)(2,1)}), bf16[4,768,1024]{2,1,0:T(8,128)(2,1)}) %all-gather.19.cloned.1.call-update) | async-done | bytes 6291472 | tf_op jit(solution)/shard_map/all_gather | solution.py:207
  1126.5 37.2 %all-gather.21.cloned.1.call-done = bf16[1536,1024]{1,0:T(8,128)(2,1)} async-done(((bf16[768,1024]{1,0:T(8,128)(2,1)}), bf16[1536,1024]{1,0:T(8,128)(2,1)}) %all-gather.21.cloned.1.call-update) | async-done | bytes 3145744 | tf_op jit(solution)/shard_map/all_gather | solution.py:207
  (239 shorter events, 322.0 us)
Async XLA Ops:
  6.5 570.2 %all-gather.9.cloned.1.call-start = ((), (), s32[]{:S(2)}) async-start(), calls=%async_computation | async-start | bytes 14450688 | tf_op jit(solution)/shard_map/all_gather | solution.py:180
  24.1 119.4 %collective-permute-start = (bf16[256,5632]{1,0:T(8,128)(2,1)}, bf16[256,5632]{1,0:T(8,128)(2,1)}, u32[]{:S(2)}, u32[]{:S(2)}) collective-permute-start(bf16[256,5632]{1,0:T(8,128)(2,1)} %constant_dynamic-slice_fusion), channel_id=1, source_target_pairs={{0,4},{4,0},{1,5},{5,1},{2,6},{6,2},{3,7},{7,3}} | collective-permute-start | bytes 8650760 | tf_op jit(solution)/shard_map/ppermute | solution.py:138
  29.4 114.1 %collective-permute-start.1 = (bf16[640,1024]{1,0:T(8,128)(2,1)S(1)}, bf16[640,1024]{1,0:T(8,128)(2,1)S(1)}, u32[]{:S(2)}, u32[]{:S(2)}) collective-permute-start(bf16[640,1024]{1,0:T(8,128)(2,1)S(1)} %fusion.77), channel_id=1, source_target_pairs={{0,4},{4,0},{1,5},{5,1},{2,6},{6,2},{3,7},{7,3}} | collective-permute-start | bytes 3932168 | tf_op jit(solution)/shard_map/ppermute | solution.py:138
  30.9 34.3 %copy-start.27 = (bf16[3072]{0:T(1024)(128)(2,1)S(1)}, bf16[3072]{0:T(1024)(128)(2,1)}, u32[]{:S(2)}) copy-start(bf16[3072]{0:T(1024)(128)(2,1)} %param.28) | copy-start | bytes 18436
  30.9 34.3 %copy-start.28 = (bf16[3072]{0:T(1024)(128)(2,1)S(1)}, bf16[3072]{0:T(1024)(128)(2,1)}, u32[]{:S(2)}) copy-start(bf16[3072]{0:T(1024)(128)(2,1)} %param.29) | copy-start | bytes 18436
  30.9 34.3 %copy-start.26 = (bf16[8192]{0:T(1024)(128)(2,1)S(1)}, bf16[8192]{0:T(1024)(128)(2,1)}, u32[]{:S(2)}) copy-start(bf16[8192]{0:T(1024)(128)(2,1)} %param.31) | copy-start | bytes 49156
  30.9 34.3 %copy-start.31 = (bf16[1024]{0:T(1024)(128)(2,1)S(1)}, bf16[1024]{0:T(1024)(128)(2,1)}, u32[]{:S(2)}) copy-start(bf16[1024]{0:T(1024)(128)(2,1)} %param.33) | copy-start | bytes 6148
  177.4 48.6 %slice-start.5 = ((s8[8388608]{0:T(1024)(128)(4,1)}), s8[4194304]{0:T(1024)(128)(4,1)S(1)}, s32[]{:S(2)}) async-start(s8[8388608]{0:T(1024)(128)(4,1)} %bitcast.136), calls=%async_computation.12 | async-start | bytes 8388608
  180.2 45.9 %copy-start.30 = (f32[1024]{0:T(1024)S(1)}, f32[1024]{0:T(1024)}, u32[]{:S(2)}) copy-start(f32[1024]{0:T(1024)} %convert_element_type.109) | copy-start | bytes 12292
  180.2 45.9 %slice-start.6 = ((s8[8388608]{0:T(1024)(128)(4,1)}), s8[4194304]{0:T(1024)(128)(4,1)S(1)}, s32[]{:S(2)}) async-start(s8[8388608]{0:T(1024)(128)(4,1)} %bitcast.136), calls=%async_computation.13 | async-start | bytes 8388608
  239.0 364.7 %all-gather.11.cloned.1.call-start = ((), (), s32[]{:S(2)}) async-start(), calls=%async_computation.1 | async-start | bytes 14450688 | tf_op jit(solution)/shard_map/all_gather | solution.py:183
  268.2 49.9 %slice-start.7 = ((s8[8388608]{0:T(1024)(128)(4,1)}), s8[4194304]{0:T(1024)(128)(4,1)S(1)}, s32[]{:S(2)}) async-start(s8[8388608]{0:T(1024)(128)(4,1)} %bitcast.138), calls=%async_computation.14 | async-start | bytes 8388608
  268.2 49.9 %slice-start.8 = ((s8[8388608]{0:T(1024)(128)(4,1)}), s8[4194304]{0:T(1024)(128)(4,1)S(1)}, s32[]{:S(2)}) async-start(s8[8388608]{0:T(1024)(128)(4,1)} %bitcast.138), calls=%async_computation.15 | async-start | bytes 8388608
  268.2 239.6 %collective-permute-start.2 = (bf16[4608,1024]{1,0:T(8,128)(2,1)}, bf16[4608,1024]{1,0:T(8,128)(2,1)}, u32[]{:S(2)}, u32[]{:S(2)}) collective-permute-start(bf16[4608,1024]{1,0:T(8,128)(2,1)} %select_select_fusion.2), channel_id=1, source_target_pairs={{0,4},{4,0},{1,5},{5,1},{2,6},{6,2},{3,7},{7,3}} | collective-permute-start | bytes 28311560 | tf_op jit(solution)/shard_map/ppermute | solution.py:176
  318.1 190.0 %copy-start.32 = (bf16[1024]{0:T(1024)(128)(2,1)S(1)}, bf16[1024]{0:T(1024)(128)(2,1)}, u32[]{:S(2)}) copy-start(bf16[1024]{0:T(1024)(128)(2,1)} %param.34) | copy-start | bytes 6148
  507.9 324.2 %all-gather.13.cloned.1.call-start = ((), (), s32[]{:S(2)}) async-start(), calls=%async_computation.2 | async-start | bytes 14417920 | tf_op jit(solution)/shard_map/all_gather | solution.py:185
  650.1 236.5 %all-gather.15.cloned.1.call-start = ((), (), s32[]{:S(2)}) async-start(), calls=%async_computation.3 | async-start | bytes 6553600 | tf_op jit(solution)/shard_map/all_gather | solution.py:186
  662.6 100.6 %copy-start.7 = (bf16[2304,1024]{1,0:T(8,128)(2,1)}, bf16[2304,1024]{1,0:T(8,128)(2,1)S(1)}, u32[]{:S(2)}) copy-start(bf16[2304,1024]{1,0:T(8,128)(2,1)S(1)} %fusion.20) | copy-start | bytes 14155780
  805.5 249.4 %all-gather.17.cloned.1.call-start = ((), (), s32[]{:S(2)}) async-start(), calls=%async_computation.4 | async-start | bytes 14155776 | tf_op jit(solution)/shard_map/all_gather | solution.py:207
  845.8 25.3 %copy-start.8 = (bf16[2304,1024]{1,0:T(8,128)(2,1)S(1)}, bf16[2304,1024]{1,0:T(8,128)(2,1)}, u32[]{:S(2)}) copy-start(bf16[2304,1024]{1,0:T(8,128)(2,1)} %copy-done.7) | copy-start | bytes 14155780
  892.9 32.3 %copy-start.18 = (bf16[768,1024]{1,0:T(8,128)(2,1)S(1)}, bf16[768,1024]{1,0:T(8,128)(2,1)}, u32[]{:S(2)}) copy-start(bf16[768,1024]{1,0:T(8,128)(2,1)} %copy-done.17) | copy-start | bytes 4718596
  925.1 195.0 %all-gather.19.cloned.1.call-start = ((), (), s32[]{:S(2)}) async-start(), calls=%async_computation.5 | async-start | bytes 9437184 | tf_op jit(solution)/shard_map/all_gather | solution.py:207
  1006.8 157.0 %all-gather.21.cloned.1.call-start = ((), (), s32[]{:S(2)}) async-start(), calls=%async_computation.6 | async-start | bytes 4718592 | tf_op jit(solution)/shard_map/all_gather | solution.py:207
  1120.1 47.5 %copy-start.1 = (s32[12,768]{1,0:T(8,128)S(1)}, s32[12,768]{1,0:T(8,128)}, u32[]{:S(2)}) copy-start(s32[12,768]{1,0:T(8,128)} %param.26) | copy-start | bytes 110596
  (29 other events, 281.3 us)
Sparse Core Ops, SparseCore 0:
  239.1 103.9 all-gather.8
  508.0 68.3 all-gather.10
  650.2 74.0 all-gather.12
  805.6 38.3 all-gather.14
  925.2 115.8 all-gather.16
  1042.5 77.5 all-gather.18
  1121.6 42.1 all-gather.20
